TPU v7x, 256 devices: a whole 4x4x8 slice. The times are simulated.
256 devices in a mesh: kv: 32 (over z, x), head: 8 (over y, core).
Axes of the slice: x: 4, y: 4, z: 8, core: 2. Of those that a mesh axis runs over, the one named last changes fastest.
Arguments:
- query: bfloat16 [2, 40, 128, 128], P(None, None, 'head'), may hold values from -16 to 16
- key_cache: bfloat16 [2, 8, 262144, 128], P(None, 'head', 'kv'), may hold values from -6 to 6
- value_cache: bfloat16 [2, 8, 262144, 128], P(None, 'head', 'kv'), may hold values from -6 to 6
- draft_keys: bfloat16 [2, 8, 40, 128], P(None, 'head'), may hold values from -12 to 12
- draft_values: bfloat16 [2, 8, 40, 128], P(None, 'head'), may hold values from -6 to 6
- lengths: int32 [2], replicated, may hold values from 32768 to 262144, as said below
- out_weight: bfloat16 [16384, 16384], P('head', 'kv'), may hold values from -0.1875 to 0.1875
Outputs:
- mixed: bfloat16 [2, 40, 16384], P(None, None, ('kv', 'head'))
Inputs may be any that keep to these rules, and one draw needn't show every extreme that they name: `lengths`: one request has exactly 262144 cached positions.
All inputs are finite; a program needn't handle non-finite values.
Results may differ from a plain program's by a relative error of at most 0.0055.
Values may be sent and summed in bfloat16 or wider, within the bound.
No kernel may reach another device: no remote copies, remote signals or barrier semaphores. Data moves between devices by JAX's collectives and lax.ppermute only.
A program may use at most 64 MiB of HBM per device.

v0:
```python
import functools
import math

import jax
import jax.numpy as jnp
from jax import lax
from jax.experimental import pallas as pl
from jax.experimental.pallas import tpu as pltpu
from jax.sharding import PartitionSpec as P

masked_score = -1e30
LANES = 128
TILE = 256
LIMIT = 2.0**120


def pair_scores(q, keys):
    return lax.dot_general(q, keys, (((1,), (1,)), ((), ())), preferred_element_type=jnp.float32)


def attend_kernel(
    lengths_ref, place_ref, q_hbm, k_hbm, v_hbm, dk_hbm, dv_hbm, out_ref,
    q_ref, k_ref, v_ref, dk_ref, dv_ref, one_ref, m_ref, mix_ref, sum_ref, sems, small_sems,
    *, factor, kv_count, span, part, block_rows,
):
    batch, rows_all, width = q_ref.shape
    local_span = k_ref.shape[1]
    draft = dk_ref.shape[1]
    group = rows_all // draft
    spans = local_span // span
    count = rows_all // part
    half_rows = rows_all // 2
    kv_index = place_ref[0]
    last = kv_index == kv_count - 1
    halves = [pl.ds(r * half_rows, half_rows) for r in range(2)]

    def small_copies():
        pairs = ((q_hbm, q_ref), (dk_hbm, dk_ref), (dv_hbm, dv_ref))
        return [pltpu.make_async_copy(a, z, small_sems.at[n]) for n, (a, z) in enumerate(pairs)]

    def span_copies(s):
        b = s // spans
        at = pl.ds(pl.multiple_of((s - b * spans) * span, span), span)
        return (
            pltpu.make_async_copy(k_hbm.at[b, at, :], k_ref.at[b, at, :], sems.at[0, s]),
            pltpu.make_async_copy(v_hbm.at[b, at, :], v_ref.at[b, at, :], sems.at[1, s]),
        )

    def start_span(s):
        for copy in span_copies(s):
            copy.start()

    def wait_span(s):
        for copy in span_copies(s):
            copy.wait()

        @pl.when(s + 2 < batch * spans)
        def _():
            start_span(s + 2)

    for copy in small_copies():
        copy.start()
    for s in range(2):
        start_span(s)
    one_ref[...] = jnp.ones(one_ref.shape, one_ref.dtype)
    for copy in small_copies():
        copy.wait()

    def reset():
        for ref, fill in ((mix_ref, 0.0), (sum_ref, 0.0), (m_ref, masked_score)):
            ref[pl.ds(0, rows_all), :] = jnp.full((rows_all, LANES), fill, jnp.float32)

    def draft_scores(b, r, rows):
        row = r * half_rows + lax.broadcasted_iota(jnp.int32, (half_rows, draft), 0)
        col = lax.broadcasted_iota(jnp.int32, (half_rows, draft), 1)
        scores = pair_scores(q_ref[b, rows, :], dk_ref[b]) * factor
        return jnp.where(col * group <= row, scores, masked_score)

    def tile_scores(b, rows, start, left):
        at = start + lax.broadcasted_iota(jnp.int32, (half_rows, TILE), 1)
        scores = pair_scores(q_ref[b, rows, :], k_ref[b, pl.ds(start, TILE), :]) * factor
        return jnp.where(at < left, scores, masked_score)

    def level_up(rows, scores):
        m_ref[rows, :] = jnp.maximum(m_ref[rows, :], jnp.max(scores, axis=1, keepdims=True))

    def add(rows, scores, values):
        weights = jnp.exp2(scores - m_ref[rows, :][:, :1]).astype(jnp.bfloat16)
        wide = jnp.concatenate([values, jnp.ones(values.shape, values.dtype)], axis=1)
        fresh = jnp.dot(weights, wide, preferred_element_type=jnp.float32)
        mix_ref[rows, :] += fresh[:, :LANES]
        sum_ref[rows, :] += fresh[:, LANES:]

    def sweep(b, i):
        for rows in halves:
            q = q_ref[b, rows, :]
            level = m_ref[rows, :]
            level = jnp.concatenate([level, level], axis=1)
            total = jnp.zeros((half_rows, 2 * LANES), jnp.float32)
            for t in range(span // TILE):
                at = pl.ds(pl.multiple_of(i * span + t * TILE, TILE), TILE)
                scores = pair_scores(q, k_ref[b, at, :]) * factor
                weights = jnp.exp2(scores - level).astype(jnp.bfloat16)
                wide = jnp.concatenate([v_ref[b, at, :], one_ref[pl.ds(t * TILE, TILE), :]], axis=1)
                total += jnp.dot(weights, wide, preferred_element_type=jnp.float32)
            mix_ref[rows, :] += total[:, :LANES]
            sum_ref[rows, :] += total[:, LANES:]

    def one_request(b, carry):
        left = lengths_ref[b] - kv_index * local_span
        reset()

        @pl.when(last)
        def _():
            for r, rows in enumerate(halves):
                level_up(rows, draft_scores(b, r, rows))

        wait_span(b * spans)

        @pl.when(left > 0)
        def _():
            for rows in halves:
                level_up(rows, tile_scores(b, rows, 0, left))

        @pl.when(last)
        def _():
            for r, rows in enumerate(halves):
                add(rows, draft_scores(b, r, rows), dv_ref[b])

        def one_span(i, carry):
            @pl.when(i > 0)
            def _():
                wait_span(b * spans + i)

            rest = left - i * span
            ragged = jnp.logical_and(rest > 0, rest < span)

            @pl.when(ragged)
            def _():
                def cut(t, carry):
                    here = pl.ds(pl.multiple_of(t * TILE, TILE), TILE)
                    there = pl.ds(pl.multiple_of(i * span + t * TILE, TILE), TILE)
                    at = t * TILE + lax.broadcasted_iota(jnp.int32, (TILE, width), 0)
                    keep = at < rest
                    kept = jnp.where(keep, v_ref[b, there, :].astype(jnp.float32), 0.0)
                    v_ref[b, there, :] = kept.astype(v_ref.dtype)
                    one_ref[here, :] = jnp.where(keep, 1.0, 0.0).astype(one_ref.dtype)
                    return carry

                lax.fori_loop(0, span // TILE, cut, 0)

            @pl.when(rest > 0)
            def _():
                sweep(b, i)

            @pl.when(ragged)
            def _():
                one_ref[...] = jnp.ones(one_ref.shape, one_ref.dtype)

            return carry

        lax.fori_loop(0, spans, one_span, 0)

        over = jnp.max(jnp.where(sum_ref[pl.ds(0, rows_all), :] < LIMIT, 0.0, 1.0))

        @pl.when(over > 0.0)
        def _():
            reset()

            def careful(rows, scores, values):
                old = m_ref[rows, :]
                level_up(rows, scores)
                shrink = jnp.exp2(old - m_ref[rows, :])
                mix_ref[rows, :] *= shrink
                sum_ref[rows, :] *= shrink
                add(rows, scores, values)

            @pl.when(last)
            def _():
                for r, rows in enumerate(halves):
                    careful(rows, draft_scores(b, r, rows), dv_ref[b])

            def step(t, carry):
                start = pl.multiple_of(t * TILE, TILE)

                @pl.when(start < left)
                def _():
                    for rows in halves:
                        careful(rows, tile_scores(b, rows, start, left), v_ref[b, pl.ds(start, TILE), :])

                return carry

            lax.fori_loop(0, local_span // TILE, step, 0)

        row = lax.broadcasted_iota(jnp.int32, (block_rows, LANES), 0)
        col = lax.broadcasted_iota(jnp.int32, (block_rows, LANES), 1)
        diagonal = jnp.logical_and(row == col, row < part)
        for d in range(count):
            rows = pl.ds(d * part, block_rows)
            total = sum_ref[rows, :]
            some = jnp.logical_and(row < part, total > 0.0)
            safe = jnp.where(some, total, 1.0)
            level = jnp.where(some, m_ref[rows, :] + jnp.log2(safe), masked_score)
            level = jnp.sum(jnp.where(diagonal, level, 0.0), axis=0, keepdims=True)
            high = level.astype(jnp.bfloat16).astype(jnp.float32)
            rest = level - high
            mid = rest.astype(jnp.bfloat16).astype(jnp.float32)
            low = rest - mid
            block = jnp.where(row < part, mix_ref[rows, :] / safe, 0.0)
            block = jnp.where(row == part, high, block)
            block = jnp.where(row == part + 1, mid, block)
            block = jnp.where(row == part + 2, low, block)
            out_ref[d, pl.ds(pl.multiple_of(b * block_rows, 8), block_rows), :] = block.astype(jnp.bfloat16)
        return carry

    lax.fori_loop(0, batch, one_request, 0)


def attend(lengths, place, q, keys, values, draft_keys, draft_values, kv_count, part, block_rows):
    batch, rows_all, width = q.shape
    local_span, draft = keys.shape[1], draft_keys.shape[1]
    span = math.gcd(local_span, 4096)
    kernel = functools.partial(
        attend_kernel, factor=math.log2(math.e) / math.sqrt(width), kv_count=kv_count,
        span=span, part=part, block_rows=block_rows,
    )
    anywhere = pl.BlockSpec(memory_space=pltpu.HBM)
    state = pltpu.VMEM((rows_all + block_rows, LANES), jnp.float32)
    out = (rows_all // part, batch * block_rows, width)
    return pl.pallas_call(
        kernel,
        out_shape=jax.ShapeDtypeStruct(out, jnp.bfloat16),
        grid_spec=pltpu.PrefetchScalarGridSpec(
            num_scalar_prefetch=2,
            grid=(1,),
            in_specs=[anywhere] * 5,
            out_specs=pl.BlockSpec(out, lambda i, *_: (0, 0, 0)),
            scratch_shapes=[
                pltpu.VMEM((batch, rows_all, width), jnp.bfloat16),
                pltpu.VMEM((batch, local_span, width), jnp.bfloat16),
                pltpu.VMEM((batch, local_span, width), jnp.bfloat16),
                pltpu.VMEM((batch, draft, width), jnp.bfloat16),
                pltpu.VMEM((batch, draft, width), jnp.bfloat16),
                pltpu.VMEM((span, LANES), jnp.bfloat16),
                state, state, state,
                pltpu.SemaphoreType.DMA((2, batch * local_span // span)),
                pltpu.SemaphoreType.DMA((3,)),
            ],
        ),
        compiler_params=pltpu.CompilerParams(vmem_limit_bytes=58 * 2**20),
        cost_estimate=pl.CostEstimate(
            flops=4 * batch * rows_all * local_span * width,
            bytes_accessed=4 * batch * local_span * width,
            transcendentals=batch * rows_all * local_span,
        ),
        name="attend",
    )(lengths, place, q, keys, values, draft_keys, draft_values)


def merge_kernel(got_ref, out_ref, both_ref, *, part, batch):
    count, rows, width = got_ref.shape
    block_rows = rows // batch
    base = (part // 8) * 8
    at = part - base
    for b in range(batch):
        stats = got_ref[:, pl.ds(b * block_rows + base, block_rows - base), :].astype(jnp.float32)
        level = stats[:, at, :] + stats[:, at + 1, :] + stats[:, at + 2, :]
        share = jnp.exp2(level - jnp.max(level, axis=0, keepdims=True))
        share = share / jnp.sum(share, axis=0, keepdims=True)
        share = share.T
        total = jnp.zeros((block_rows, width), jnp.float32)
        for s in range(count):
            mine = got_ref[s, pl.ds(b * block_rows, block_rows), :].astype(jnp.float32)
            total = total + share[:block_rows, s : s + 1] * mine
        both_ref[pl.ds(b * part, block_rows), :] = total
    done = both_ref[pl.ds(0, batch * part), :].astype(out_ref.dtype)
    for s in range(count):
        out_ref[s] = done


def merge(got, part, batch):
    count, rows, width = got.shape
    return pl.pallas_call(
        functools.partial(merge_kernel, part=part, batch=batch),
        out_shape=jax.ShapeDtypeStruct((count, batch * part, width), jnp.bfloat16),
        scratch_shapes=[pltpu.VMEM((rows, width), jnp.float32)],
        compiler_params=pltpu.CompilerParams(vmem_limit_bytes=8 * 2**20),
        name="merge",
    )(got)


def project_kernel(a_ref, w_ref, out_ref, rows_ref, *, group, heads, batch):
    count, both, width = a_ref.shape
    part = both // batch
    draft = count * part // group
    cycle = math.lcm(group, part)
    steps = count * part // cycle
    half = width // 2
    for d in range(count):
        rows_ref[pl.ds(d * both, both), :] = a_ref[d].astype(jnp.float32)
    rows = []
    for b in range(batch):
        for j in range(cycle // group):
            line = []
            for g in range(group):
                d, r = divmod(j * group + g, part)
                at = pl.ds(d * both + b * part + r, steps, stride=cycle * batch)
                line.append(rows_ref[at, :])
            rows.append(jnp.concatenate(line, axis=1))
    rows = jnp.concatenate(rows, axis=0).astype(jnp.bfloat16)
    product = jnp.dot(rows, w_ref[...], preferred_element_type=jnp.float32)
    lane = lax.broadcasted_iota(jnp.int32, (draft, width), 1)
    for c in range(heads // 2):
        one = product[:draft, c * width : (c + 1) * width]
        two = product[draft:, c * width : (c + 1) * width]
        out_ref[2 * c] = jnp.where(lane < half, one, pltpu.roll(two, half, 1)).astype(out_ref.dtype)
        out_ref[2 * c + 1] = jnp.where(lane < half, pltpu.roll(one, half, 1), two).astype(out_ref.dtype)


def per_device(query, key_cache, value_cache, draft_keys, draft_values, lengths, out_weight):
    batch, draft, group, width = query.shape
    kv_count = lax.axis_size("kv")
    heads = lax.axis_size("head")
    local_span = key_cache.shape[2]
    part = draft * group // kv_count
    block_rows = -(-(part + 3) // 8) * 8
    place = lax.axis_index("kv").astype(jnp.int32)[None]
    exchange = functools.partial(lax.all_to_all, split_axis=0, concat_axis=0, tiled=True)
    sent = attend(
        lengths, place,
        query.reshape(batch, draft * group, width),
        key_cache.reshape(batch, local_span, width),
        value_cache.reshape(batch, local_span, width),
        draft_keys.reshape(batch, draft, width),
        draft_values.reshape(batch, draft, width),
        kv_count, part, block_rows,
    )
    everyone = exchange(merge(exchange(sent, "kv"), part, batch), "kv")
    shares = pl.pallas_call(
        functools.partial(project_kernel, group=group, heads=heads, batch=batch),
        out_shape=jax.ShapeDtypeStruct((heads, draft, width), jnp.bfloat16),
        scratch_shapes=[pltpu.VMEM((kv_count * batch * part, width), jnp.float32)],
        compiler_params=pltpu.CompilerParams(vmem_limit_bytes=16 * 2**20),
        name="project",
    )(everyone, out_weight)
    arrived = exchange(shares, "head")
    cycle = math.lcm(group, part) // group
    mixed = jnp.sum(arrived.astype(jnp.float32), axis=0)
    mixed = mixed.reshape(cycle, draft // cycle, batch, width // 2)
    mixed = jnp.transpose(mixed, (2, 1, 0, 3)).reshape(batch, draft, width // 2)
    return mixed.astype(jnp.bfloat16)


def solution(mesh):
    in_specs = (
        P(None, None, "head", None),
        P(None, "head", "kv", None),
        P(None, "head", "kv", None),
        P(None, "head", None, None),
        P(None, "head", None, None),
        P(),
        P("head", "kv"),
    )
    out_specs = P(None, None, ("kv", "head"))
    return jax.shard_map(
        per_device, mesh=mesh, in_specs=in_specs, out_specs=out_specs, check_vma=False
    )
```

profile of v0, /device:TPU:1, one launch (start us, length us, event | category | flops | bytes accessed | tf_op | source)
XLA Modules:
  0.0 124.5 jit_solution(9250161844128413311)
XLA Ops:
  0.0 0.0 copy-start
  0.0 17.5 %attend.1 = bf16[32,48,128]{2,1,0:T(8,128)(2,1)} custom-call(s32[2]{0:T(128)} %lengths_ref.1, s32[1]{0:T(128)} %bitcast.place_ref, bf16[2,640,128]{2,1,0:T(8,128)(2,1)} %bitcast.12, bf16[2,8192,128]{2,1,0:T(8,128)(2,1)} %bitcast.10, bf16[2,8192,128]{2,1,0:T(8,128)(2,1)} %bitcast.11, bf16[2,40,128]{2,1,0:T(8,128)(2,1)} %bitcast.13, bf16[2,40,128]{2,1,0:T(8,128)(2,1)} %bitcast.14), custom_call_target="tpu_custom_call" | custom-call | flops 5368709120 | bytes 8388608 | tf_op jit(solution)/shard_map/attend/pallas_call | solution.py:230
  17.5 73.2 %all_to_all.15.got_ref = bf16[32,48,128]{2,1,0:T(8,128)(2,1)S(1)} all-to-all(bf16[32,48,128]{2,1,0:T(8,128)(2,1)} %attend.1), channel_id=1, replica_groups=mesh['kv'=32,'head'=8] {'kv'}, dimensions={0} | all-to-all | bytes 786432 | tf_op jit(solution)/shard_map/all_to_all | solution.py:338
  90.7 0.5 merge.1
  91.2 16.3 %all_to_all.16.a_ref = bf16[32,40,128]{2,1,0:T(8,128)(2,1)S(1)} all-to-all(bf16[32,40,128]{2,1,0:T(8,128)(2,1)S(1)} %merge.1), channel_id=1, replica_groups=mesh['kv'=32,'head'=8] {'kv'}, dimensions={0} | all-to-all | bytes 655360 | tf_op jit(solution)/shard_map/all_to_all | solution.py:338
  107.5 0.0 copy-done
  107.5 0.7 project.1
  108.2 15.5 %all_to_all.17 = bf16[8,40,128]{2,1,0:T(8,128)(2,1)S(1)} all-to-all(bf16[8,40,128]{2,1,0:T(8,128)(2,1)S(1)} %project.1), channel_id=1, replica_groups=mesh['kv'=32,'head'=8] {'head'}, dimensions={0} | all-to-all | bytes 163840 | tf_op jit(solution)/shard_map/all_to_all | solution.py:346
  123.7 0.1 convert_element_type.11
  123.8 0.6 copy.9
  (2 shorter events, 0.0 us)
Async XLA Ops:
  0.0 107.5 %copy-start = (bf16[2048,512]{1,0:T(8,128)(2,1)S(1)}, bf16[2048,512]{1,0:T(8,128)(2,1)}, u32[]{:S(2)}) copy-start(bf16[2048,512]{1,0:T(8,128)(2,1)} %w_ref.1) | copy-start | bytes 6291460
where the time goes:
time: 125 us; the launch traced here: 124 us
  blocking collectives  105 us (84%)
  Pallas kernels  18.7 us (15%)
    all_to_all x2, blocking collectives, per_device(): everyone = exchange(merge(exchange(sent, 'kv'), part, batch), 'kv')  89.5 us
    pallas_call x1, Pallas kernels, attend(): pl.pallas_call(kernel, out_shape=jax.ShapeDtypeStruct(out, jnp.bfloat16),...  17.5 us
    all_to_all x1, blocking collectives, per_device(): arrived = exchange(shares, 'head')  15.5 us

commit v1 on v0

--- a/solution.py
+++ b/solution.py
@@ -19,8 +19,8 @@
 
 
 def attend_kernel(
-    lengths_ref, place_ref, q_hbm, k_hbm, v_hbm, dk_hbm, dv_hbm, out_ref,
-    q_ref, k_ref, v_ref, dk_ref, dv_ref, one_ref, m_ref, mix_ref, sum_ref, sems, small_sems,
+    place_ref, lengths_hbm, q_hbm, k_hbm, v_hbm, dk_hbm, dv_hbm, out_ref,
+    lengths_ref, q_ref, k_ref, v_ref, dk_ref, dv_ref, one_ref, m_ref, mix_ref, sum_ref, sems, small_sems,
     *, factor, kv_count, span, part, block_rows,
 ):
     batch, rows_all, width = q_ref.shape
@@ -35,7 +35,7 @@
     halves = [pl.ds(r * half_rows, half_rows) for r in range(2)]
 
     def small_copies():
-        pairs = ((q_hbm, q_ref), (dk_hbm, dk_ref), (dv_hbm, dv_ref))
+        pairs = ((q_hbm, q_ref), (lengths_hbm, lengths_ref), (dk_hbm, dk_ref), (dv_hbm, dv_ref))
         return [pltpu.make_async_copy(a, z, small_sems.at[n]) for n, (a, z) in enumerate(pairs)]
 
     def span_copies(s):
@@ -47,24 +47,21 @@
         )
 
     def start_span(s):
-        for copy in span_copies(s):
-            copy.start()
-
-    def wait_span(s):
-        for copy in span_copies(s):
-            copy.wait()
-
-        @pl.when(s + 2 < batch * spans)
-        def _():
-            start_span(s + 2)
-
-    for copy in small_copies():
+        @pl.when(s < batch * spans)
+        def _():
+            for copy in span_copies(s):
+                copy.start()
+
+    for copy in small_copies()[:2]:
         copy.start()
-    for s in range(2):
-        start_span(s)
+    for copy in span_copies(0):
+        copy.start()
+    for copy in small_copies()[2:]:
+        copy.start()
     one_ref[...] = jnp.ones(one_ref.shape, one_ref.dtype)
     for copy in small_copies():
         copy.wait()
+    start_span(1)
 
     def reset():
         for ref, fill in ((mix_ref, 0.0), (sum_ref, 0.0), (m_ref, masked_score)):
@@ -115,7 +112,8 @@
             for r, rows in enumerate(halves):
                 level_up(rows, draft_scores(b, r, rows))
 
-        wait_span(b * spans)
+        span_copies(b * spans)[0].wait()
+        start_span(b * spans + 2)
 
         @pl.when(left > 0)
         def _():
@@ -130,7 +128,10 @@
         def one_span(i, carry):
             @pl.when(i > 0)
             def _():
-                wait_span(b * spans + i)
+                span_copies(b * spans + i)[0].wait()
+                start_span(b * spans + i + 2)
+
+            span_copies(b * spans + i)[1].wait()
 
             rest = left - i * span
             ragged = jnp.logical_and(rest > 0, rest < span)
@@ -219,7 +220,7 @@
 def attend(lengths, place, q, keys, values, draft_keys, draft_values, kv_count, part, block_rows):
     batch, rows_all, width = q.shape
     local_span, draft = keys.shape[1], draft_keys.shape[1]
-    span = math.gcd(local_span, 4096)
+    span = math.gcd(local_span, 2048)
     kernel = functools.partial(
         attend_kernel, factor=math.log2(math.e) / math.sqrt(width), kv_count=kv_count,
         span=span, part=part, block_rows=block_rows,
@@ -231,11 +232,12 @@
         kernel,
         out_shape=jax.ShapeDtypeStruct(out, jnp.bfloat16),
         grid_spec=pltpu.PrefetchScalarGridSpec(
-            num_scalar_prefetch=2,
+            num_scalar_prefetch=1,
             grid=(1,),
-            in_specs=[anywhere] * 5,
+            in_specs=[anywhere] * 6,
             out_specs=pl.BlockSpec(out, lambda i, *_: (0, 0, 0)),
             scratch_shapes=[
+                pltpu.SMEM((batch,), jnp.int32),
                 pltpu.VMEM((batch, rows_all, width), jnp.bfloat16),
                 pltpu.VMEM((batch, local_span, width), jnp.bfloat16),
                 pltpu.VMEM((batch, local_span, width), jnp.bfloat16),
@@ -244,7 +246,7 @@
                 pltpu.VMEM((span, LANES), jnp.bfloat16),
                 state, state, state,
                 pltpu.SemaphoreType.DMA((2, batch * local_span // span)),
-                pltpu.SemaphoreType.DMA((3,)),
+                pltpu.SemaphoreType.DMA((4,)),
             ],
         ),
         compiler_params=pltpu.CompilerParams(vmem_limit_bytes=58 * 2**20),
@@ -254,7 +256,7 @@
             transcendentals=batch * rows_all * local_span,
         ),
         name="attend",
-    )(lengths, place, q, keys, values, draft_keys, draft_values)
+    )(place, lengths, q, keys, values, draft_keys, draft_values)
 
 
 def merge_kernel(got_ref, out_ref, both_ref, *, part, batch):

time: 125 us -> 125 us (level)
    all_to_all x1, blocking collectives: 15.5 us -> 10.1 us  [per_device(): arrived = exchange(shares, 'head')]
    all_to_all x2, blocking collectives: 89.5 us -> 94.2 us  [per_device(): everyone = exchange(merge(exchange(sent, 'kv'), part, batch), 'kv')]
where the time goes in v1:
time: 125 us; the launch traced here: 124 us
  blocking collectives  104 us (83%)
  Pallas kernels  19.1 us (15%)
    all_to_all x2, blocking collectives, per_device(): everyone = exchange(merge(exchange(sent, 'kv'), part, batch), 'kv')  94.2 us
    pallas_call x1, Pallas kernels, attend(): pl.pallas_call(kernel, out_shape=jax.ShapeDtypeStruct(out, jnp.bfloat16),...  17.9 us
    all_to_all x1, blocking collectives, per_device(): arrived = exchange(shares, 'head')  10.1 us

profile of v1, /device:TPU:1, one launch (start us, length us, event | category | flops | bytes accessed | tf_op | source)
XLA Modules:
  0.0 124.1 jit_solution(8776248148029802880)
XLA Ops:
  0.0 0.0 copy-start
  0.0 17.9 %attend.1 = bf16[32,48,128]{2,1,0:T(8,128)(2,1)} custom-call(s32[1]{0:T(128)} %bitcast.place_ref, s32[2]{0:T(128)} %lengths_hbm.1, bf16[2,640,128]{2,1,0:T(8,128)(2,1)} %bitcast.12, bf16[2,8192,128]{2,1,0:T(8,128)(2,1)} %bitcast.10, bf16[2,8192,128]{2,1,0:T(8,128)(2,1)} %bitcast.11, bf16[2,40,128]{2,1,0:T(8,128)(2,1)} %bitcast.13, bf16[2,40,128]{2,1,0:T(8,128)(2,1)} %bitcast.14), custom_call_target="tpu_custom_call" | custom-call | flops 5368709120 | bytes 8388608 | tf_op jit(solution)/shard_map/attend/pallas_call | solution.py:231
  17.9 77.2 %all_to_all.15.got_ref = bf16[32,48,128]{2,1,0:T(8,128)(2,1)S(1)} all-to-all(bf16[32,48,128]{2,1,0:T(8,128)(2,1)} %attend.1), channel_id=1, replica_groups=mesh['kv'=32,'head'=8] {'kv'}, dimensions={0} | all-to-all | bytes 786432 | tf_op jit(solution)/shard_map/all_to_all | solution.py:340
  95.0 0.5 merge.1
  95.6 17.0 %all_to_all.16.a_ref = bf16[32,40,128]{2,1,0:T(8,128)(2,1)S(1)} all-to-all(bf16[32,40,128]{2,1,0:T(8,128)(2,1)S(1)} %merge.1), channel_id=1, replica_groups=mesh['kv'=32,'head'=8] {'kv'}, dimensions={0} | all-to-all | bytes 655360 | tf_op jit(solution)/shard_map/all_to_all | solution.py:340
  112.6 0.0 copy-done
  112.6 0.7 project.1
  113.3 10.1 %all_to_all.17 = bf16[8,40,128]{2,1,0:T(8,128)(2,1)S(1)} all-to-all(bf16[8,40,128]{2,1,0:T(8,128)(2,1)S(1)} %project.1), channel_id=1, replica_groups=mesh['kv'=32,'head'=8] {'head'}, dimensions={0} | all-to-all | bytes 163840 | tf_op jit(solution)/shard_map/all_to_all | solution.py:348
  123.4 0.1 convert_element_type.11
  123.5 0.6 copy.9
  (2 shorter events, 0.0 us)
Async XLA Ops:
  0.0 112.6 %copy-start = (bf16[2048,512]{1,0:T(8,128)(2,1)S(1)}, bf16[2048,512]{1,0:T(8,128)(2,1)}, u32[]{:S(2)}) copy-start(bf16[2048,512]{1,0:T(8,128)(2,1)} %w_ref.1) | copy-start | bytes 6291460

commit v2 on v1

--- a/solution.py
+++ b/solution.py
@@ -88,17 +88,40 @@
         mix_ref[rows, :] += fresh[:, :LANES]
         sum_ref[rows, :] += fresh[:, LANES:]
 
-    def sweep(b, i):
-        for rows in halves:
+    def ready(b, c, left):
+        s = b * spans + c
+        if c > 0:
+            span_copies(s)[0].wait()
+            start_span(s + 2)
+        span_copies(s)[1].wait()
+        rest = left - c * span
+
+        @pl.when(rest < span)
+        def _():
+            def cut(t, carry):
+                here = pl.ds(pl.multiple_of(c * span + t * TILE, TILE), TILE)
+                at = t * TILE + lax.broadcasted_iota(jnp.int32, (TILE, width), 0)
+                keep = at < rest
+                kept = jnp.where(keep, v_ref[b, here, :].astype(jnp.float32), 0.0)
+                v_ref[b, here, :] = kept.astype(v_ref.dtype)
+                one_ref[here, :] = jnp.where(keep, 1.0, 0.0).astype(one_ref.dtype)
+                return carry
+
+            lax.fori_loop(0, span // TILE, cut, 0)
+
+    def sweep(b, left):
+        for r, rows in enumerate(halves):
             q = q_ref[b, rows, :]
             level = m_ref[rows, :]
             level = jnp.concatenate([level, level], axis=1)
             total = jnp.zeros((half_rows, 2 * LANES), jnp.float32)
-            for t in range(span // TILE):
-                at = pl.ds(pl.multiple_of(i * span + t * TILE, TILE), TILE)
+            for t in range(local_span // TILE):
+                if r == 0 and t * TILE % span == 0:
+                    ready(b, t * TILE // span, left)
+                at = pl.ds(t * TILE, TILE)
                 scores = pair_scores(q, k_ref[b, at, :]) * factor
                 weights = jnp.exp2(scores - level).astype(jnp.bfloat16)
-                wide = jnp.concatenate([v_ref[b, at, :], one_ref[pl.ds(t * TILE, TILE), :]], axis=1)
+                wide = jnp.concatenate([v_ref[b, at, :], one_ref[at, :]], axis=1)
                 total += jnp.dot(weights, wide, preferred_element_type=jnp.float32)
             mix_ref[rows, :] += total[:, :LANES]
             sum_ref[rows, :] += total[:, LANES:]
@@ -125,42 +148,21 @@
             for r, rows in enumerate(halves):
                 add(rows, draft_scores(b, r, rows), dv_ref[b])
 
-        def one_span(i, carry):
-            @pl.when(i > 0)
-            def _():
-                span_copies(b * spans + i)[0].wait()
-                start_span(b * spans + i + 2)
-
-            span_copies(b * spans + i)[1].wait()
-
-            rest = left - i * span
-            ragged = jnp.logical_and(rest > 0, rest < span)
-
-            @pl.when(ragged)
-            def _():
-                def cut(t, carry):
-                    here = pl.ds(pl.multiple_of(t * TILE, TILE), TILE)
-                    there = pl.ds(pl.multiple_of(i * span + t * TILE, TILE), TILE)
-                    at = t * TILE + lax.broadcasted_iota(jnp.int32, (TILE, width), 0)
-                    keep = at < rest
-                    kept = jnp.where(keep, v_ref[b, there, :].astype(jnp.float32), 0.0)
-                    v_ref[b, there, :] = kept.astype(v_ref.dtype)
-                    one_ref[here, :] = jnp.where(keep, 1.0, 0.0).astype(one_ref.dtype)
-                    return carry
-
-                lax.fori_loop(0, span // TILE, cut, 0)
-
-            @pl.when(rest > 0)
-            def _():
-                sweep(b, i)
-
-            @pl.when(ragged)
+        @pl.when(left > 0)
+        def _():
+            sweep(b, left)
+
+            @pl.when(left < local_span)
             def _():
                 one_ref[...] = jnp.ones(one_ref.shape, one_ref.dtype)
 
-            return carry
-
-        lax.fori_loop(0, spans, one_span, 0)
+        @pl.when(left <= 0)
+        def _():
+            for c in range(spans):
+                if c > 0:
+                    span_copies(b * spans + c)[0].wait()
+                    start_span(b * spans + c + 2)
+                span_copies(b * spans + c)[1].wait()
 
         over = jnp.max(jnp.where(sum_ref[pl.ds(0, rows_all), :] < LIMIT, 0.0, 1.0))
 
@@ -220,7 +222,7 @@
 def attend(lengths, place, q, keys, values, draft_keys, draft_values, kv_count, part, block_rows):
     batch, rows_all, width = q.shape
     local_span, draft = keys.shape[1], draft_keys.shape[1]
-    span = math.gcd(local_span, 2048)
+    span = math.gcd(local_span, 4096)
     kernel = functools.partial(
         attend_kernel, factor=math.log2(math.e) / math.sqrt(width), kv_count=kv_count,
         span=span, part=part, block_rows=block_rows,
@@ -243,7 +245,7 @@
                 pltpu.VMEM((batch, local_span, width), jnp.bfloat16),
                 pltpu.VMEM((batch, draft, width), jnp.bfloat16),
                 pltpu.VMEM((batch, draft, width), jnp.bfloat16),
-                pltpu.VMEM((span, LANES), jnp.bfloat16),
+                pltpu.VMEM((local_span, LANES), jnp.bfloat16),
                 state, state, state,
                 pltpu.SemaphoreType.DMA((2, batch * local_span // span)),
                 pltpu.SemaphoreType.DMA((4,)),

time: 125 us -> 123 us (0.984)
  blocking collectives: 104 us -> 47.6 us
  Pallas kernels: 19.1 us -> 74.4 us
    all_to_all x2, blocking collectives: 94.2 us -> 33.7 us  [per_device(): everyone = exchange(merge(exchange(sent, 'kv'), part, batch), 'kv')]
    pallas_call x1, Pallas kernels: 17.9 us -> 73.2 us  [attend(): pl.pallas_call(kernel, out_shape=jax.ShapeDtypeStruct(out, jnp.bfloat16),...]
    all_to_all x1, blocking collectives: 10.1 us -> 13.9 us  [per_device(): arrived = exchange(shares, 'head')]
where the time goes in v2:
time: 123 us
  Pallas kernels  74.4 us (60%)
  blocking collectives  47.6 us (39%)
    pallas_call x1, Pallas kernels, attend(): pl.pallas_call(kernel, out_shape=jax.ShapeDtypeStruct(out, jnp.bfloat16),...  73.2 us
    all_to_all x2, blocking collectives, per_device(): everyone = exchange(merge(exchange(sent, 'kv'), part, batch), 'kv')  33.7 us
    all_to_all x1, blocking collectives, per_device(): arrived = exchange(shares, 'head')  13.9 us

profile of v2, /device:TPU:1, one launch (start us, length us, event | category | flops | bytes accessed | tf_op | source)
XLA Modules:
  0.0 122.8 jit_solution(12624438372341818760)
XLA Ops:
  0.0 0.0 copy-start
  0.0 73.2 %attend.1 = bf16[32,48,128]{2,1,0:T(8,128)(2,1)} custom-call(s32[1]{0:T(128)} %bitcast.place_ref, s32[2]{0:T(128)} %lengths_hbm.1, bf16[2,640,128]{2,1,0:T(8,128)(2,1)} %bitcast.12, bf16[2,8192,128]{2,1,0:T(8,128)(2,1)} %bitcast.10, bf16[2,8192,128]{2,1,0:T(8,128)(2,1)} %bitcast.11, bf16[2,40,128]{2,1,0:T(8,128)(2,1)} %bitcast.13, bf16[2,40,128]{2,1,0:T(8,128)(2,1)} %bitcast.14), custom_call_target="tpu_custom_call" | custom-call | flops 5368709120 | bytes 8388608 | tf_op jit(solution)/shard_map/attend/pallas_call | solution.py:233
  73.2 17.6 %all_to_all.15.got_ref = bf16[32,48,128]{2,1,0:T(8,128)(2,1)S(1)} all-to-all(bf16[32,48,128]{2,1,0:T(8,128)(2,1)} %attend.1), channel_id=1, replica_groups=mesh['kv'=32,'head'=8] {'kv'}, dimensions={0} | all-to-all | bytes 786432 | tf_op jit(solution)/shard_map/all_to_all | solution.py:342
  90.8 0.5 merge.1
  91.3 16.1 %all_to_all.16.a_ref = bf16[32,40,128]{2,1,0:T(8,128)(2,1)S(1)} all-to-all(bf16[32,40,128]{2,1,0:T(8,128)(2,1)S(1)} %merge.1), channel_id=1, replica_groups=mesh['kv'=32,'head'=8] {'kv'}, dimensions={0} | all-to-all | bytes 655360 | tf_op jit(solution)/shard_map/all_to_all | solution.py:342
  107.4 0.0 copy-done
  107.4 0.7 project.1
  108.1 13.9 %all_to_all.17 = bf16[8,40,128]{2,1,0:T(8,128)(2,1)S(1)} all-to-all(bf16[8,40,128]{2,1,0:T(8,128)(2,1)S(1)} %project.1), channel_id=1, replica_groups=mesh['kv'=32,'head'=8] {'head'}, dimensions={0} | all-to-all | bytes 163840 | tf_op jit(solution)/shard_map/all_to_all | solution.py:350
  122.0 0.1 convert_element_type.11
  122.1 0.6 copy.9
  (2 shorter events, 0.0 us)
Async XLA Ops:
  0.0 107.4 %copy-start = (bf16[2048,512]{1,0:T(8,128)(2,1)S(1)}, bf16[2048,512]{1,0:T(8,128)(2,1)}, u32[]{:S(2)}) copy-start(bf16[2048,512]{1,0:T(8,128)(2,1)} %w_ref.1) | copy-start | bytes 6291460

commit v3 on v2

--- a/solution.py
+++ b/solution.py
@@ -20,7 +20,7 @@
 
 def attend_kernel(
     place_ref, lengths_hbm, q_hbm, k_hbm, v_hbm, dk_hbm, dv_hbm, out_ref,
-    lengths_ref, q_ref, k_ref, v_ref, dk_ref, dv_ref, one_ref, m_ref, mix_ref, sum_ref, sems, small_sems,
+    out_s, lengths_ref, q_ref, k_ref, v_ref, dk_ref, dv_ref, one_ref, m_ref, mix_ref, sum_ref, sems, small_sems, out_sems,
     *, factor, kv_count, span, part, block_rows,
 ):
     batch, rows_all, width = q_ref.shape
@@ -29,10 +29,10 @@
     group = rows_all // draft
     spans = local_span // span
     count = rows_all // part
-    half_rows = rows_all // 2
+    half_rows = rows_all
     kv_index = place_ref[0]
     last = kv_index == kv_count - 1
-    halves = [pl.ds(r * half_rows, half_rows) for r in range(2)]
+    halves = [pl.ds(r * half_rows, half_rows) for r in range(1)]
 
     def small_copies():
         pairs = ((q_hbm, q_ref), (lengths_hbm, lengths_ref), (dk_hbm, dk_ref), (dv_hbm, dv_ref))
@@ -213,10 +213,17 @@
             block = jnp.where(row == part, high, block)
             block = jnp.where(row == part + 1, mid, block)
             block = jnp.where(row == part + 2, low, block)
-            out_ref[d, pl.ds(pl.multiple_of(b * block_rows, 8), block_rows), :] = block.astype(jnp.bfloat16)
+            out_s[b, d] = block.astype(jnp.bfloat16)
+        out_copy(b).start()
         return carry
 
+    def out_copy(b):
+        there = pl.ds(pl.multiple_of(b * block_rows, 8), block_rows)
+        return pltpu.make_async_copy(out_s.at[b], out_ref.at[:, there, :], out_sems.at[b])
+
     lax.fori_loop(0, batch, one_request, 0)
+    for b in range(batch):
+        out_copy(b).wait()
 
 
 def attend(lengths, place, q, keys, values, draft_keys, draft_values, kv_count, part, block_rows):
@@ -237,8 +244,9 @@
             num_scalar_prefetch=1,
             grid=(1,),
             in_specs=[anywhere] * 6,
-            out_specs=pl.BlockSpec(out, lambda i, *_: (0, 0, 0)),
+            out_specs=anywhere,
             scratch_shapes=[
+                pltpu.VMEM((batch, rows_all // part, block_rows, width), jnp.bfloat16),
                 pltpu.SMEM((batch,), jnp.int32),
                 pltpu.VMEM((batch, rows_all, width), jnp.bfloat16),
                 pltpu.VMEM((batch, local_span, width), jnp.bfloat16),
@@ -249,6 +257,7 @@
                 state, state, state,
                 pltpu.SemaphoreType.DMA((2, batch * local_span // span)),
                 pltpu.SemaphoreType.DMA((4,)),
+                pltpu.SemaphoreType.DMA((batch,)),
             ],
         ),
         compiler_params=pltpu.CompilerParams(vmem_limit_bytes=58 * 2**20),

time: 123 us -> 123 us (level)
  blocking collectives: 47.6 us -> 76.3 us
  Pallas kernels: 74.4 us -> 45.9 us
    all_to_all x1, blocking collectives: 13.9 us -> 45.2 us  [per_device(): arrived = exchange(shares, 'head')]
    pallas_call x1, Pallas kernels: 73.2 us -> 44.7 us  [attend(): pl.pallas_call(kernel, out_shape=jax.ShapeDtypeStruct(out, jnp.bfloat16),...]
    all_to_all x2, blocking collectives: 33.7 us -> 31.1 us  [per_device(): everyone = exchange(merge(exchange(sent, 'kv'), part, batch), 'kv')]
where the time goes in v3:
time: 123 us
  blocking collectives  76.3 us (62%)
  Pallas kernels  45.9 us (37%)
    all_to_all x1, blocking collectives, per_device(): arrived = exchange(shares, 'head')  45.2 us
    pallas_call x1, Pallas kernels, attend(): pl.pallas_call(kernel, out_shape=jax.ShapeDtypeStruct(out, jnp.bfloat16),...  44.7 us
    all_to_all x2, blocking collectives, per_device(): everyone = exchange(merge(exchange(sent, 'kv'), part, batch), 'kv')  31.1 us

profile of v3, /device:TPU:1, one launch (start us, length us, event | category | flops | bytes accessed | tf_op | source)
XLA Modules:
  0.0 123.0 jit_solution(5114531456947459904)
XLA Ops:
  0.0 0.0 copy-start
  0.0 44.7 %attend.1 = bf16[32,48,128]{2,1,0:T(8,128)(2,1)} custom-call(s32[1]{0:T(128)} %bitcast.place_ref, s32[2]{0:T(128)} %lengths_hbm.1, bf16[2,640,128]{2,1,0:T(8,128)(2,1)} %bitcast.12, bf16[2,8192,128]{2,1,0:T(8,128)(2,1)} %bitcast.10, bf16[2,8192,128]{2,1,0:T(8,128)(2,1)} %bitcast.11, bf16[2,40,128]{2,1,0:T(8,128)(2,1)} %bitcast.13, bf16[2,40,128]{2,1,0:T(8,128)(2,1)} %bitcast.14), custom_call_target="tpu_custom_call" | custom-call | flops 5368709120 | bytes 8388608 | tf_op jit(solution)/shard_map/attend/pallas_call | solution.py:240
  44.7 16.7 %all_to_all.15.got_ref = bf16[32,48,128]{2,1,0:T(8,128)(2,1)S(1)} all-to-all(bf16[32,48,128]{2,1,0:T(8,128)(2,1)} %attend.1), channel_id=1, replica_groups=mesh['kv'=32,'head'=8] {'kv'}, dimensions={0} | all-to-all | bytes 786432 | tf_op jit(solution)/shard_map/all_to_all | solution.py:351
  61.4 0.5 merge.1
  61.9 14.4 %all_to_all.16.a_ref = bf16[32,40,128]{2,1,0:T(8,128)(2,1)S(1)} all-to-all(bf16[32,40,128]{2,1,0:T(8,128)(2,1)S(1)} %merge.1), channel_id=1, replica_groups=mesh['kv'=32,'head'=8] {'kv'}, dimensions={0} | all-to-all | bytes 655360 | tf_op jit(solution)/shard_map/all_to_all | solution.py:351
  76.3 0.0 copy-done
  76.3 0.7 project.1
  77.0 45.2 %all_to_all.17 = bf16[8,40,128]{2,1,0:T(8,128)(2,1)S(1)} all-to-all(bf16[8,40,128]{2,1,0:T(8,128)(2,1)S(1)} %project.1), channel_id=1, replica_groups=mesh['kv'=32,'head'=8] {'head'}, dimensions={0} | all-to-all | bytes 163840 | tf_op jit(solution)/shard_map/all_to_all | solution.py:359
  122.2 0.1 convert_element_type.11
  122.3 0.6 copy.9
  (2 shorter events, 0.0 us)
Async XLA Ops:
  0.0 76.3 %copy-start = (bf16[2048,512]{1,0:T(8,128)(2,1)S(1)}, bf16[2048,512]{1,0:T(8,128)(2,1)}, u32[]{:S(2)}) copy-start(bf16[2048,512]{1,0:T(8,128)(2,1)} %w_ref.1) | copy-start | bytes 6291460
